TPU v7x, 256 devices: a whole 4x4x8 slice. The times are simulated.
256 devices in a mesh: trial: 4 (over z_lo), lat: 2 (over z_hi), lon: 4 (over x_hi, core), lev: 8 (over y, x_lo).
Axes of the slice: x: 4 (x_hi: 2, x_lo: 2; x = x_hi * 2 + x_lo), y: 4, z: 8 (z_hi: 2, z_lo: 4; z = z_hi * 4 + z_lo), core: 2. Of those that a mesh axis runs over, the one named last changes fastest.
Arguments:
- density: float32 [32, 64, 1024, 128], P(('trial', 'lat'), 'lon', 'lev'), parts along dimension 0, may hold values from 0.5 to 2
- crowding: float32 [32, 64, 1024, 128], P(('trial', 'lat'), 'lon', 'lev'), parts along dimension 0, may hold values from 0.5 to 2
Outputs:
- scaled_field: float32 [32, 64, 1024, 128], P(('trial', 'lat'), 'lon', 'lev'), parts along dimension 0
- density_end: float32 [32, 64, 1024, 128], P(('trial', 'lat'), 'lon', 'lev'), parts along dimension 0
There are 4 independent parts, one for each index of `trial`. A program takes and returns all parts, laid end to end along the dimension named above; each array names one. Nothing has to cross between parts.
All inputs are finite; a program needn't handle non-finite values.
Results may differ from a plain program's by a relative error of at most 0.000058.
Values sent between devices are 32-bit elements; how exact they have to be, the bound alone decides.
A program may use at most 64 MiB of HBM per device.

v0:
```python
import jax
import jax.numpy as jnp
from jax import lax
from jax.sharding import PartitionSpec as P

STEPS = 4


def with_halo(array, sides, width):
    edges = {}
    for axis, dim in sides:
        devices, length = (lax.axis_size(axis), array.shape[dim])
        up = [(i, (i + 1) % devices) for i in range(devices - 1)]
        last = lax.slice_in_dim(array, length - width, length, axis=dim)
        first = lax.slice_in_dim(array, 0, width, axis=dim)
        edges[dim] = (
            lax.ppermute(last, axis, up),
            lax.ppermute(first, axis, [(b, a) for a, b in up]),
        )
    done = []
    for _, dim in sides:
        low, high = edges[dim]
        around = [(width, width) if d in done else (0, 0) for d in range(array.ndim)]
        array = jnp.concatenate([jnp.pad(low, around), array, jnp.pad(high, around)], axis=dim)
        done.append(dim)
    return array


def from_everyone(array, axis):
    devices = lax.axis_size(axis)
    return lax.all_to_all(
        jnp.broadcast_to(array[None], (devices, *array.shape)), axis, 0, 0, tiled=True
    )


def taken_together(array, axis):
    everything = from_everyone(array, axis)
    return jnp.sum(everything, axis=0)


def in_one(arrays, axis):
    line, at, done = (jnp.concatenate([a.reshape(-1) for a in arrays]), 0, [])
    so_far = taken_together(line, axis)
    for a in arrays:
        done.append(so_far[at : at + a.size].reshape(a.shape))
        at += a.size
    return tuple(done)


def inner_cells(values, dims):
    for dim in dims:
        values = lax.slice_in_dim(values, 1, values.shape[dim] - 1, axis=dim)
    return values


def side_cells(values, dim, start, dims):
    others = [other for other in dims if other != dim]
    values = inner_cells(values, others)
    return lax.slice_in_dim(values, start, start + values.shape[dim] - 2, axis=dim)


def advance(padded, crowding):
    middle = inner_cells(padded, (0, 1, 2))
    lower = [side_cells(padded, dim, 0, (0, 1, 2)) for dim in (0, 1, 2)]
    upper = [side_cells(padded, dim, 2, (0, 1, 2)) for dim in (0, 1, 2)]
    spread = lower[0] + upper[0] + lower[1] + upper[1] + lower[2] + upper[2] - 6.0 * middle
    return middle + 0.1 * spread + 0.2 * middle * (1.0 - middle * crowding)


def shards(density, crowding):
    for step in range(STEPS):
        padded = with_halo(density, (("lat", 0), ("lon", 1), ("lev", 2)), 1)
        density = advance(padded, crowding)
    count = density.shape[1] * lax.axis_size("lon")
    guess = 1.0
    moved = density - guess
    totals, squares = in_one(
        (jnp.sum(moved, axis=1, keepdims=True), jnp.sum(moved * moved, axis=1, keepdims=True)),
        "lon",
    )
    line_mean = guess + totals / count
    centred = density - line_mean
    line_variance = squares / count - totals / count * (totals / count)
    scaled_field = centred * lax.rsqrt(line_variance + 0.0001)
    return (scaled_field, density)


def solution(mesh):
    placed = (P(("trial", "lat"), "lon", "lev", None), P(("trial", "lat"), "lon", "lev", None))
    return jax.shard_map(
        shards,
        mesh=mesh,
        in_specs=placed,
        out_specs=(
            P(("trial", "lat"), "lon", "lev", None),
            P(("trial", "lat"), "lon", "lev", None),
        ),
        check_vma=False,
    )
```

profile of v0, /device:TPU:1, one launch (start us, length us, event | category | flops | bytes accessed | tf_op | source)
XLA Modules:
  0.0 274.8 jit_solution(10510386888826523579)
XLA Ops:
  0.6 1.8 fusion.60
  2.5 9.8 %collective-permute-start = (f32[1,16,128,128]{3,2,1,0:T(8,128)S(1)}, f32[1,16,128,128]{3,2,1,0:T(8,128)S(1)}, u32[]{:S(2)}, u32[]{:S(2)}) collective-permute-start(f32[1,16,128,128]{3,2,1,0:T(8,128)S(1)} %get-tuple-element.28), channel_id=1, source_target_pairs={{0,32},{1,33},{2,34},{3,35},{4,36},{5,37},{6,38},{7,39},{8,40},{9,... | collective-permute-start | bytes 3145736 | tf_op jit(solution)/shard_map/ppermute | solution.py:17
  13.7 5.5 %collective-permute-start.2 = (f32[4,1,128,128]{3,2,1,0:T(8,128)S(1)}, f32[4,1,128,128]{3,2,1,0:T(8,128)S(1)}, u32[]{:S(2)}, u32[]{:S(2)}) collective-permute-start(f32[4,1,128,128]{3,2,1,0:T(8,128)S(1)} %get-tuple-element.25), channel_id=1, source_target_pairs={{0,8},{8,16},{16,24},{1,9},{9,17},{17,25},{2,10},{10,18},{18,26},{... | collective-permute-start | bytes 786440 | tf_op jit(solution)/shard_map/ppermute | solution.py:17
  19.2 1.9 collective-permute-start.3
  21.2 2.2 collective-permute-start.4
  24.7 3.9 %collective-permute-done.3 = f32[4,1,128,128]{3,2,1,0:T(8,128)S(1)} collective-permute-done((f32[4,1,128,128]{3,2,1,0:T(8,128)S(1)}, f32[4,1,128,128]{3,2,1,0:T(8,128)S(1)}, u32[]{:S(2)}, u32[]{:S(2)}) %collective-permute-start.3) | collective-permute-done | bytes 262176 | tf_op jit(solution)/shard_map/ppermute | solution.py:18
  28.7 10.0 %collective-permute-done = f32[1,16,128,128]{3,2,1,0:T(8,128)S(1)} collective-permute-done((f32[1,16,128,128]{3,2,1,0:T(8,128)S(1)}, f32[1,16,128,128]{3,2,1,0:T(8,128)S(1)}, u32[]{:S(2)}, u32[]{:S(2)}) %collective-permute-start) | collective-permute-done | bytes 1048608 | tf_op jit(solution)/shard_map/ppermute | solution.py:17
  39.8 2.4 constant_dynamic-update-slice_fusion.1
  42.2 21.4 %collective-permute-done.1 = f32[1,16,128,128]{3,2,1,0:T(8,128)S(1)} collective-permute-done((f32[1,16,128,128]{3,2,1,0:T(8,128)S(1)}, f32[1,16,128,128]{3,2,1,0:T(8,128)S(1)}, u32[]{:S(2)}, u32[]{:S(2)}) %collective-permute-start.1) | collective-permute-done | bytes 1048608 | tf_op jit(solution)/shard_map/ppermute | solution.py:18
  64.8 9.2 %fusion.38 = f32[4,16,128,128]{3,2,1,0:T(8,128)S(1)} fusion(f32[4,16,128,128]{3,2,1,0:T(8,128)S(1)} %copy-done.1, f32[4,16,1,128]{3,2,1,0:T(1,128)S(1)} %collective-permute-done.5, f32[6,1,128,128]{3,2,1,0:T(8,128)S(1)} %pad.51, f32[6,16,128,128]{3,2,1,0:T(8,128)} %constant_dynamic-update-slice_fusion, f32[6,1,128,128]{3,2,1,0:T(8,128)S(1)} %pad.50, ...), kind=kLoop, calls=%fused_computation.93 | loop fusion | flops 31457280 | bytes 21823488 | tf_op jit(solution)/shard_map/add | solution.py:67
  74.2 1.4 collective-permute-start.6
  76.9 6.5 %collective-permute-start.8 = (f32[4,1,128,128]{3,2,1,0:T(8,128)S(1)}, f32[4,1,128,128]{3,2,1,0:T(8,128)S(1)}, u32[]{:S(2)}, u32[]{:S(2)}) collective-permute-start(f32[4,1,128,128]{3,2,1,0:T(8,128)S(1)} %get-tuple-element.21), channel_id=1, source_target_pairs={{0,8},{8,16},{16,24},{1,9},{9,17},{17,25},{2,10},{10,18},{18,26},{... | collective-permute-start | bytes 786440 | tf_op jit(solution)/shard_map/ppermute | solution.py:17
  83.5 1.9 collective-permute-start.9
  85.4 2.2 collective-permute-start.10
  89.0 3.9 %collective-permute-done.9 = f32[4,1,128,128]{3,2,1,0:T(8,128)S(1)} collective-permute-done((f32[4,1,128,128]{3,2,1,0:T(8,128)S(1)}, f32[4,1,128,128]{3,2,1,0:T(8,128)S(1)}, u32[]{:S(2)}, u32[]{:S(2)}) %collective-permute-start.9) | collective-permute-done | bytes 262176 | tf_op jit(solution)/shard_map/ppermute | solution.py:18
  93.3 3.1 %collective-permute-done.6 = f32[1,16,128,128]{3,2,1,0:T(8,128)S(1)} collective-permute-done((f32[1,16,128,128]{3,2,1,0:T(8,128)S(1)}, f32[1,16,128,128]{3,2,1,0:T(8,128)S(1)}, u32[]{:S(2)}, u32[]{:S(2)}) %collective-permute-start.6) | collective-permute-done | bytes 1048608 | tf_op jit(solution)/shard_map/ppermute | solution.py:17
  96.4 7.9 %collective-permute-done.7 = f32[1,16,128,128]{3,2,1,0:T(8,128)S(1)} collective-permute-done((f32[1,16,128,128]{3,2,1,0:T(8,128)S(1)}, f32[1,16,128,128]{3,2,1,0:T(8,128)S(1)}, u32[]{:S(2)}, u32[]{:S(2)}) %collective-permute-start.7) | collective-permute-done | bytes 1048608 | tf_op jit(solution)/shard_map/ppermute | solution.py:18
  104.4 8.1 %fusion.27 = f32[4,16,128,128]{3,2,1,0:T(8,128)S(1)} fusion(f32[4,16,128,128]{3,2,1,0:T(8,128)S(1)} %fusion.38, f32[4,16,1,128]{3,2,1,0:T(1,128)S(1)} %collective-permute-done.11, f32[6,1,128,128]{3,2,1,0:T(8,128)S(1)} %pad.55, f32[6,1,128,128]{3,2,1,0:T(8,128)S(1)} %pad.54, f32[1,16,128,128]{3,2,1,0:T(8,128)S(1)} %collective-permute-done.7, ...), kind=kLoop, calls=%fused_computation.64 | loop fusion | flops 39845888 | bytes 15532032 | tf_op jit(solution)/shard_map/add | solution.py:67
  115.3 31.9 %collective-permute-start.14 = (f32[4,1,128,128]{3,2,1,0:T(8,128)S(1)}, f32[4,1,128,128]{3,2,1,0:T(8,128)S(1)}, u32[]{:S(2)}, u32[]{:S(2)}) collective-permute-start(f32[4,1,128,128]{3,2,1,0:T(8,128)S(1)} %get-tuple-element.15), channel_id=1, source_target_pairs={{0,8},{8,16},{16,24},{1,9},{9,17},{17,25},{2,10},{10,18},{18,26},{... | collective-permute-start | bytes 786440 | tf_op jit(solution)/shard_map/ppermute | solution.py:17
  147.2 1.9 collective-permute-start.15
  149.2 2.2 collective-permute-start.16
  152.8 3.9 %collective-permute-done.15 = f32[4,1,128,128]{3,2,1,0:T(8,128)S(1)} collective-permute-done((f32[4,1,128,128]{3,2,1,0:T(8,128)S(1)}, f32[4,1,128,128]{3,2,1,0:T(8,128)S(1)}, u32[]{:S(2)}, u32[]{:S(2)}) %collective-permute-start.15) | collective-permute-done | bytes 262176 | tf_op jit(solution)/shard_map/ppermute | solution.py:18
  157.1 8.1 %fusion.16 = f32[4,16,128,128]{3,2,1,0:T(8,128)S(1)} fusion(f32[4,16,128,128]{3,2,1,0:T(8,128)S(1)} %fusion.27, f32[4,16,1,128]{3,2,1,0:T(1,128)S(1)} %collective-permute-done.17, f32[6,1,128,128]{3,2,1,0:T(8,128)S(1)} %pad.59, f32[6,1,128,128]{3,2,1,0:T(8,128)S(1)} %pad.58, f32[1,16,128,128]{3,2,1,0:T(8,128)S(1)} %collective-permute-done.13, ...), kind=kLoop, calls=%fused_computation.35 | loop fusion | flops 39845888 | bytes 15532032 | tf_op jit(solution)/shard_map/add | solution.py:67
  165.4 8.3 %collective-permute-start.18 = (f32[1,16,128,128]{3,2,1,0:T(8,128)S(1)}, f32[1,16,128,128]{3,2,1,0:T(8,128)S(1)}, u32[]{:S(2)}, u32[]{:S(2)}) collective-permute-start(f32[1,16,128,128]{3,2,1,0:T(8,128)S(1)} %get-tuple-element.9), channel_id=1, source_target_pairs={{0,32},{1,33},{2,34},{3,35},{4,36},{5,37},{6,38},{7,39},{8,40},{9,... | collective-permute-start | bytes 3145736 | tf_op jit(solution)/shard_map/ppermute | solution.py:17
  175.1 27.3 %collective-permute-start.20 = (f32[4,1,128,128]{3,2,1,0:T(8,128)S(1)}, f32[4,1,128,128]{3,2,1,0:T(8,128)S(1)}, u32[]{:S(2)}, u32[]{:S(2)}) collective-permute-start(f32[4,1,128,128]{3,2,1,0:T(8,128)S(1)} %get-tuple-element.7), channel_id=1, source_target_pairs={{0,8},{8,16},{16,24},{1,9},{9,17},{17,25},{2,10},{10,18},{18,26},{... | collective-permute-start | bytes 786440 | tf_op jit(solution)/shard_map/ppermute | solution.py:17
  202.4 1.9 collective-permute-start.21
  207.0 4.6 %collective-permute-done.21 = f32[4,1,128,128]{3,2,1,0:T(8,128)S(1)} collective-permute-done((f32[4,1,128,128]{3,2,1,0:T(8,128)S(1)}, f32[4,1,128,128]{3,2,1,0:T(8,128)S(1)}, u32[]{:S(2)}, u32[]{:S(2)}) %collective-permute-start.21) | collective-permute-done | bytes 262176 | tf_op jit(solution)/shard_map/ppermute | solution.py:18
  212.0 4.6 %collective-permute-done.19 = f32[1,16,128,128]{3,2,1,0:T(8,128)S(1)} collective-permute-done((f32[1,16,128,128]{3,2,1,0:T(8,128)S(1)}, f32[1,16,128,128]{3,2,1,0:T(8,128)S(1)}, u32[]{:S(2)}, u32[]{:S(2)}) %collective-permute-start.19) | collective-permute-done | bytes 1048608 | tf_op jit(solution)/shard_map/ppermute | solution.py:18
  216.6 9.5 %add_reduce_fusion = (f32[4,128,128]{2,1,0:T(8,128)S(1)}, f32[4,128,128]{2,1,0:T(8,128)S(1)}, f32[4,16,128,128]{3,2,1,0:T(8,128)}) fusion(f32[4,16,128,128]{3,2,1,0:T(8,128)S(1)} %fusion.16, f32[4,16,128,128]{3,2,1,0:T(8,128)S(1)} %copy-done, f32[4,16,1,128]{3,2,1,0:T(1,128)S(1)} %collective-permute-done.23, f32[6,1,128,128]{3,2,1,0:T(8,128)S(1)} %pad.63, ...), kind=kLoop, calls=%fused_computation.112 | loop fusion | flops 43909120 | bytes 16056320 | tf_op jit(solution)/shard_map/reduce_sum | solution.py:78
  227.2 40.6 %all_to_all.6 = f32[4,1,131072]{2,1,0:T(1,128)S(1)} all-to-all(f32[4,1,131072]{2,1,0:T(1,128)S(1)} %broadcast_in_dim.2), channel_id=1, replica_groups=mesh['trial'=4,'lat'=2,'lon'=4,'lev'=8] {'lon'}, dimensions={0} | all-to-all | bytes 4194304 | tf_op jit(solution)/shard_map/all_to_all | solution.py:31
  267.8 1.9 reduce_sum.29
  269.8 5.0 %subtract_multiply_fusion = f32[4,16,128,128]{3,2,1,0:T(8,128)} fusion(f32[4,16,128,128]{3,2,1,0:T(8,128)} %get-tuple-element.4, f32[4,128,128]{2,1,0:T(8,128)S(1)} %bitcast.7, f32[4,128,128]{2,1,0:T(8,128)S(1)} %bitcast.6), kind=kLoop, calls=%fused_computation.110 | loop fusion | flops 2097152 | bytes 8912896 | tf_op jit(solution)/shard_map/mul | solution.py:84
  (55 shorter events, 18.8 us)
Async XLA Ops:
  0.6 13.0 %copy-start.1 = (f32[4,16,128,128]{3,2,1,0:T(8,128)S(1)}, f32[4,16,128,128]{3,2,1,0:T(8,128)}, u32[]{:S(2)}) copy-start(f32[4,16,128,128]{3,2,1,0:T(8,128)} %param.2) | copy-start | bytes 12582916
  2.5 36.2 %collective-permute-start = (f32[1,16,128,128]{3,2,1,0:T(8,128)S(1)}, f32[1,16,128,128]{3,2,1,0:T(8,128)S(1)}, u32[]{:S(2)}, u32[]{:S(2)}) collective-permute-start(f32[1,16,128,128]{3,2,1,0:T(8,128)S(1)} %get-tuple-element.28), channel_id=1, source_target_pairs={{0,32},{1,33},{2,34},{3,35},{4,36},{5,37},{6,38},{7,39},{8,40},{9,... | collective-permute-start | bytes 3145736 | tf_op jit(solution)/shard_map/ppermute | solution.py:17
  12.3 51.2 %collective-permute-start.1 = (f32[1,16,128,128]{3,2,1,0:T(8,128)S(1)}, f32[1,16,128,128]{3,2,1,0:T(8,128)S(1)}, u32[]{:S(2)}, u32[]{:S(2)}) collective-permute-start(f32[1,16,128,128]{3,2,1,0:T(8,128)S(1)} %get-tuple-element.27), channel_id=1, source_target_pairs={{32,0},{33,1},{34,2},{35,3},{36,4},{37,5},{38,6},{39,7},{40,8},{41... | collective-permute-start | bytes 3145736 | tf_op jit(solution)/shard_map/ppermute | solution.py:18
  13.7 9.7 %collective-permute-start.2 = (f32[4,1,128,128]{3,2,1,0:T(8,128)S(1)}, f32[4,1,128,128]{3,2,1,0:T(8,128)S(1)}, u32[]{:S(2)}, u32[]{:S(2)}) collective-permute-start(f32[4,1,128,128]{3,2,1,0:T(8,128)S(1)} %get-tuple-element.25), channel_id=1, source_target_pairs={{0,8},{8,16},{16,24},{1,9},{9,17},{17,25},{2,10},{10,18},{18,26},{... | collective-permute-start | bytes 786440 | tf_op jit(solution)/shard_map/ppermute | solution.py:17
  19.2 9.5 %collective-permute-start.3 = (f32[4,1,128,128]{3,2,1,0:T(8,128)S(1)}, f32[4,1,128,128]{3,2,1,0:T(8,128)S(1)}, u32[]{:S(2)}, u32[]{:S(2)}) collective-permute-start(f32[4,1,128,128]{3,2,1,0:T(8,128)S(1)} %get-tuple-element.26), channel_id=1, source_target_pairs={{8,0},{16,8},{24,16},{9,1},{17,9},{25,17},{10,2},{18,10},{26,18},{... | collective-permute-start | bytes 786440 | tf_op jit(solution)/shard_map/ppermute | solution.py:18
  21.2 43.5 %collective-permute-start.4 = (f32[4,16,1,128]{3,2,1,0:T(1,128)S(1)}, f32[4,16,1,128]{3,2,1,0:T(1,128)S(1)}, u32[]{:S(2)}, u32[]{:S(2)}) collective-permute-start(f32[4,16,1,128]{3,2,1,0:T(1,128)S(1)} %get-tuple-element.23), channel_id=1, source_target_pairs={{0,1},{1,2},{2,3},{3,4},{4,5},{5,6},{6,7},{8,9},{9,10},{10,11},{11... | collective-permute-start | bytes 98312 | tf_op jit(solution)/shard_map/ppermute | solution.py:17
  23.4 41.5 %collective-permute-start.5 = (f32[4,16,1,128]{3,2,1,0:T(1,128)S(1)}, f32[4,16,1,128]{3,2,1,0:T(1,128)S(1)}, u32[]{:S(2)}, u32[]{:S(2)}) collective-permute-start(f32[4,16,1,128]{3,2,1,0:T(1,128)S(1)} %get-tuple-element.24), channel_id=1, source_target_pairs={{1,0},{2,1},{3,2},{4,3},{5,4},{6,5},{7,6},{9,8},{10,9},{11,10},{12... | collective-permute-start | bytes 98312 | tf_op jit(solution)/shard_map/ppermute | solution.py:18
  39.8 25.1 %copy-start = (f32[4,16,128,128]{3,2,1,0:T(8,128)S(1)}, f32[4,16,128,128]{3,2,1,0:T(8,128)}, u32[]{:S(2)}) copy-start(f32[4,16,128,128]{3,2,1,0:T(8,128)} %param.3) | copy-start | bytes 12582916
  63.5 1.3 copy-start.2
  74.2 22.2 %collective-permute-start.6 = (f32[1,16,128,128]{3,2,1,0:T(8,128)S(1)}, f32[1,16,128,128]{3,2,1,0:T(8,128)S(1)}, u32[]{:S(2)}, u32[]{:S(2)}) collective-permute-start(f32[1,16,128,128]{3,2,1,0:T(8,128)S(1)} %get-tuple-element.19), channel_id=1, source_target_pairs={{0,32},{1,33},{2,34},{3,35},{4,36},{5,37},{6,38},{7,39},{8,40},{9,... | collective-permute-start | bytes 3145736 | tf_op jit(solution)/shard_map/ppermute | solution.py:17
  75.6 28.8 %collective-permute-start.7 = (f32[1,16,128,128]{3,2,1,0:T(8,128)S(1)}, f32[1,16,128,128]{3,2,1,0:T(8,128)S(1)}, u32[]{:S(2)}, u32[]{:S(2)}) collective-permute-start(f32[1,16,128,128]{3,2,1,0:T(8,128)S(1)} %get-tuple-element.20), channel_id=1, source_target_pairs={{32,0},{33,1},{34,2},{35,3},{36,4},{37,5},{38,6},{39,7},{40,8},{41... | collective-permute-start | bytes 3145736 | tf_op jit(solution)/shard_map/ppermute | solution.py:18
  76.9 10.7 %collective-permute-start.8 = (f32[4,1,128,128]{3,2,1,0:T(8,128)S(1)}, f32[4,1,128,128]{3,2,1,0:T(8,128)S(1)}, u32[]{:S(2)}, u32[]{:S(2)}) collective-permute-start(f32[4,1,128,128]{3,2,1,0:T(8,128)S(1)} %get-tuple-element.21), channel_id=1, source_target_pairs={{0,8},{8,16},{16,24},{1,9},{9,17},{17,25},{2,10},{10,18},{18,26},{... | collective-permute-start | bytes 786440 | tf_op jit(solution)/shard_map/ppermute | solution.py:17
  83.5 9.5 %collective-permute-start.9 = (f32[4,1,128,128]{3,2,1,0:T(8,128)S(1)}, f32[4,1,128,128]{3,2,1,0:T(8,128)S(1)}, u32[]{:S(2)}, u32[]{:S(2)}) collective-permute-start(f32[4,1,128,128]{3,2,1,0:T(8,128)S(1)} %get-tuple-element.22), channel_id=1, source_target_pairs={{8,0},{16,8},{24,16},{9,1},{17,9},{25,17},{10,2},{18,10},{26,18},{... | collective-permute-start | bytes 786440 | tf_op jit(solution)/shard_map/ppermute | solution.py:18
  85.4 7.5 %collective-permute-start.10 = (f32[4,16,1,128]{3,2,1,0:T(1,128)S(1)}, f32[4,16,1,128]{3,2,1,0:T(1,128)S(1)}, u32[]{:S(2)}, u32[]{:S(2)}) collective-permute-start(f32[4,16,1,128]{3,2,1,0:T(1,128)S(1)} %get-tuple-element.17), channel_id=1, source_target_pairs={{0,1},{1,2},{2,3},{3,4},{4,5},{5,6},{6,7},{8,9},{9,10},{10,11},{11... | collective-permute-start | bytes 98312 | tf_op jit(solution)/shard_map/ppermute | solution.py:17
  87.7 5.7 %collective-permute-start.11 = (f32[4,16,1,128]{3,2,1,0:T(1,128)S(1)}, f32[4,16,1,128]{3,2,1,0:T(1,128)S(1)}, u32[]{:S(2)}, u32[]{:S(2)}) collective-permute-start(f32[4,16,1,128]{3,2,1,0:T(1,128)S(1)} %get-tuple-element.18), channel_id=1, source_target_pairs={{1,0},{2,1},{3,2},{4,3},{5,4},{6,5},{7,6},{9,8},{10,9},{11,10},{12... | collective-permute-start | bytes 98312 | tf_op jit(solution)/shard_map/ppermute | solution.py:18
  112.6 44.5 %collective-permute-start.12 = (f32[1,16,128,128]{3,2,1,0:T(8,128)S(1)}, f32[1,16,128,128]{3,2,1,0:T(8,128)S(1)}, u32[]{:S(2)}, u32[]{:S(2)}) collective-permute-start(f32[1,16,128,128]{3,2,1,0:T(8,128)S(1)} %get-tuple-element.13), channel_id=1, source_target_pairs={{0,32},{1,33},{2,34},{3,35},{4,36},{5,37},{6,38},{7,39},{8,40},{9,... | collective-permute-start | bytes 3145736 | tf_op jit(solution)/shard_map/ppermute | solution.py:17
  114.0 43.1 %collective-permute-start.13 = (f32[1,16,128,128]{3,2,1,0:T(8,128)S(1)}, f32[1,16,128,128]{3,2,1,0:T(8,128)S(1)}, u32[]{:S(2)}, u32[]{:S(2)}) collective-permute-start(f32[1,16,128,128]{3,2,1,0:T(8,128)S(1)} %get-tuple-element.14), channel_id=1, source_target_pairs={{32,0},{33,1},{34,2},{35,3},{36,4},{37,5},{38,6},{39,7},{40,8},{41... | collective-permute-start | bytes 3145736 | tf_op jit(solution)/shard_map/ppermute | solution.py:18
  115.3 36.1 %collective-permute-start.14 = (f32[4,1,128,128]{3,2,1,0:T(8,128)S(1)}, f32[4,1,128,128]{3,2,1,0:T(8,128)S(1)}, u32[]{:S(2)}, u32[]{:S(2)}) collective-permute-start(f32[4,1,128,128]{3,2,1,0:T(8,128)S(1)} %get-tuple-element.15), channel_id=1, source_target_pairs={{0,8},{8,16},{16,24},{1,9},{9,17},{17,25},{2,10},{10,18},{18,26},{... | collective-permute-start | bytes 786440 | tf_op jit(solution)/shard_map/ppermute | solution.py:17
  147.2 9.5 %collective-permute-start.15 = (f32[4,1,128,128]{3,2,1,0:T(8,128)S(1)}, f32[4,1,128,128]{3,2,1,0:T(8,128)S(1)}, u32[]{:S(2)}, u32[]{:S(2)}) collective-permute-start(f32[4,1,128,128]{3,2,1,0:T(8,128)S(1)} %get-tuple-element.16), channel_id=1, source_target_pairs={{8,0},{16,8},{24,16},{9,1},{17,9},{25,17},{10,2},{18,10},{26,18},{... | collective-permute-start | bytes 786440 | tf_op jit(solution)/shard_map/ppermute | solution.py:18
  149.2 7.5 %collective-permute-start.16 = (f32[4,16,1,128]{3,2,1,0:T(1,128)S(1)}, f32[4,16,1,128]{3,2,1,0:T(1,128)S(1)}, u32[]{:S(2)}, u32[]{:S(2)}) collective-permute-start(f32[4,16,1,128]{3,2,1,0:T(1,128)S(1)} %get-tuple-element.11), channel_id=1, source_target_pairs={{0,1},{1,2},{2,3},{3,4},{4,5},{5,6},{6,7},{8,9},{9,10},{10,11},{11... | collective-permute-start | bytes 98312 | tf_op jit(solution)/shard_map/ppermute | solution.py:17
  151.4 5.7 %collective-permute-start.17 = (f32[4,16,1,128]{3,2,1,0:T(1,128)S(1)}, f32[4,16,1,128]{3,2,1,0:T(1,128)S(1)}, u32[]{:S(2)}, u32[]{:S(2)}) collective-permute-start(f32[4,16,1,128]{3,2,1,0:T(1,128)S(1)} %get-tuple-element.12), channel_id=1, source_target_pairs={{1,0},{2,1},{3,2},{4,3},{5,4},{6,5},{7,6},{9,8},{10,9},{11,10},{12... | collective-permute-start | bytes 98312 | tf_op jit(solution)/shard_map/ppermute | solution.py:18
  165.4 46.5 %collective-permute-start.18 = (f32[1,16,128,128]{3,2,1,0:T(8,128)S(1)}, f32[1,16,128,128]{3,2,1,0:T(8,128)S(1)}, u32[]{:S(2)}, u32[]{:S(2)}) collective-permute-start(f32[1,16,128,128]{3,2,1,0:T(8,128)S(1)} %get-tuple-element.9), channel_id=1, source_target_pairs={{0,32},{1,33},{2,34},{3,35},{4,36},{5,37},{6,38},{7,39},{8,40},{9,... | collective-permute-start | bytes 3145736 | tf_op jit(solution)/shard_map/ppermute | solution.py:17
  173.8 42.8 %collective-permute-start.19 = (f32[1,16,128,128]{3,2,1,0:T(8,128)S(1)}, f32[1,16,128,128]{3,2,1,0:T(8,128)S(1)}, u32[]{:S(2)}, u32[]{:S(2)}) collective-permute-start(f32[1,16,128,128]{3,2,1,0:T(8,128)S(1)} %get-tuple-element.10), channel_id=1, source_target_pairs={{32,0},{33,1},{34,2},{35,3},{36,4},{37,5},{38,6},{39,7},{40,8},{41... | collective-permute-start | bytes 3145736 | tf_op jit(solution)/shard_map/ppermute | solution.py:18
  175.1 30.6 %collective-permute-start.20 = (f32[4,1,128,128]{3,2,1,0:T(8,128)S(1)}, f32[4,1,128,128]{3,2,1,0:T(8,128)S(1)}, u32[]{:S(2)}, u32[]{:S(2)}) collective-permute-start(f32[4,1,128,128]{3,2,1,0:T(8,128)S(1)} %get-tuple-element.7), channel_id=1, source_target_pairs={{0,8},{8,16},{16,24},{1,9},{9,17},{17,25},{2,10},{10,18},{18,26},{... | collective-permute-start | bytes 786440 | tf_op jit(solution)/shard_map/ppermute | solution.py:17
  202.4 9.2 %collective-permute-start.21 = (f32[4,1,128,128]{3,2,1,0:T(8,128)S(1)}, f32[4,1,128,128]{3,2,1,0:T(8,128)S(1)}, u32[]{:S(2)}, u32[]{:S(2)}) collective-permute-start(f32[4,1,128,128]{3,2,1,0:T(8,128)S(1)} %get-tuple-element.8), channel_id=1, source_target_pairs={{8,0},{16,8},{24,16},{9,1},{17,9},{25,17},{10,2},{18,10},{26,18},{... | collective-permute-start | bytes 786440 | tf_op jit(solution)/shard_map/ppermute | solution.py:18
  204.4 7.2 %collective-permute-start.22 = (f32[4,16,1,128]{3,2,1,0:T(1,128)S(1)}, f32[4,16,1,128]{3,2,1,0:T(1,128)S(1)}, u32[]{:S(2)}, u32[]{:S(2)}) collective-permute-start(f32[4,16,1,128]{3,2,1,0:T(1,128)S(1)} %get-tuple-element.5), channel_id=1, source_target_pairs={{0,1},{1,2},{2,3},{3,4},{4,5},{5,6},{6,7},{8,9},{9,10},{10,11},{11... | collective-permute-start | bytes 98312 | tf_op jit(solution)/shard_map/ppermute | solution.py:17
  205.7 6.3 %collective-permute-start.23 = (f32[4,16,1,128]{3,2,1,0:T(1,128)S(1)}, f32[4,16,1,128]{3,2,1,0:T(1,128)S(1)}, u32[]{:S(2)}, u32[]{:S(2)}) collective-permute-start(f32[4,16,1,128]{3,2,1,0:T(1,128)S(1)} %get-tuple-element.6), channel_id=1, source_target_pairs={{1,0},{2,1},{3,2},{4,3},{5,4},{6,5},{7,6},{9,8},{10,9},{11,10},{12... | collective-permute-start | bytes 98312 | tf_op jit(solution)/shard_map/ppermute | solution.py:18
where the time goes:
time: 276 us; the launch traced here: 275 us
  starting transfers between devices  118 us (43%)
  waiting for transfers between devices  64.5 us (23%)
  other arithmetic  41.9 us (15%)
  blocking collectives  40.6 us (15%)
  local copies, waits for them, and re-layouts  8.81 us (3%)
    ppermute x12, starting transfers between devices, with_halo(): lax.ppermute(last, axis, up)  99.9 us
    ppermute x12, waiting for transfers between devices, with_halo(): lax.ppermute(first, axis, [(b, a) for a, b in up])  51.3 us
    all_to_all x1, blocking collectives, from_everyone(): lax.all_to_all(jnp.broadcast_to(array[None], (devices, *array.shape)), ax...  40.6 us
    add x3, other arithmetic, advance(): return middle + 0.1 * spread + 0.2 * middle * (1.0 - middle * crowding)  25.3 us
    ppermute x12, starting transfers between devices, with_halo(): lax.ppermute(first, axis, [(b, a) for a, b in up])  18 us
    ppermute x12, waiting for transfers between devices, with_halo(): lax.ppermute(last, axis, up)  13.2 us
    reduce_sum x1, other arithmetic, shards(): jnp.sum(moved, axis=1, keepdims=True)  9.51 us
  transfers between devices with their start and end apart: 24, of which 12 were waited for; matrix products, arithmetic and copies ran while one was open for 2% of the time, Pallas kernels for 0%

commit v1 on v0

v1 whole, which is shorter than its diff:
```python
import functools

import jax
import jax.numpy as jnp
from jax import lax
from jax.experimental import pallas as pl
from jax.experimental.pallas import tpu as pltpu
from jax.sharding import PartitionSpec as P

STEPS = 4
TILE = 8
MESH = pl.DeviceIdType.MESH


def kernel(
    devices, shape, density, crowding, scaled_out, density_out,
    field, crowd, beyond, stats, load_sems,
    lat_send, lat_recv, lon_send, lon_recv, lev_send, lev_recv, stat_send, stat_recv,
):
    rows, wide, deep, _ = shape
    slabs = deep // TILE
    lat, lon, lev = (lax.axis_index(a) for a in ("lat", "lon", "lev"))
    lons, levs = devices["lon"], devices["lev"]

    def own_row(row):
        return lat * row + (1 - lat) * (rows - 1 - row)

    def slab_at(place):
        odd = place % 2
        return odd * (slabs - 1) + (1 - 2 * odd) * (place // 2)

    def inner(slab):
        return pl.ds(pl.multiple_of(slab * TILE, TILE), TILE)

    def padded(slab):
        return pl.ds(pl.multiple_of((slab + 1) * TILE, TILE), TILE)

    def lat_copy(parity, slab):
        return pltpu.make_async_remote_copy(
            src_ref=field.at[parity, 0, pl.ds(1, wide), padded(slab)],
            dst_ref=beyond.at[parity, :, inner(slab)],
            send_sem=lat_send.at[parity, slab],
            recv_sem=lat_recv.at[parity, slab],
            device_id={"lat": 1 - lat},
            device_id_type=MESH,
        )

    def lon_copy(parity, slab, up):
        return pltpu.make_async_remote_copy(
            src_ref=field.at[parity, :, wide if up else 1, padded(slab)],
            dst_ref=field.at[parity, :, 0 if up else wide + 1, padded(slab)],
            send_sem=lon_send.at[up, parity, slab],
            recv_sem=lon_recv.at[up, parity, slab],
            device_id={"lon": lon + (1 if up else -1)},
            device_id_type=MESH,
        )

    def lev_copy(parity, up):
        return pltpu.make_async_remote_copy(
            src_ref=field.at[parity, :, pl.ds(1, wide), pl.ds(deep if up else TILE, TILE)],
            dst_ref=field.at[parity, :, pl.ds(1, wide), pl.ds(0 if up else deep + TILE, TILE)],
            send_sem=lev_send.at[up, parity],
            recv_sem=lev_recv.at[up, parity],
            device_id={"lev": lev + (1 if up else -1)},
            device_id_type=MESH,
        )

    def stat_copy(slab, peer, source):
        return pltpu.make_async_remote_copy(
            src_ref=stats.at[slab, source],
            dst_ref=stats.at[slab, source],
            send_sem=stat_send.at[slab, peer],
            recv_sem=stat_recv.at[slab, source],
            device_id={"lon": peer},
            device_id_type=MESH,
        )

    def to_sides(slab, act):
        pl.when(lon > 0)(lambda: act(lambda parity: lon_copy(parity, slab, 0)))
        pl.when(lon < lons - 1)(lambda: act(lambda parity: lon_copy(parity, slab, 1)))
        pl.when((slab == 0) & (lev > 0))(lambda: act(lambda parity: lev_copy(parity, 0)))
        pl.when((slab == slabs - 1) & (lev < levs - 1))(lambda: act(lambda parity: lev_copy(parity, 1)))

    def from_sides(slab, act):
        pl.when(lon < lons - 1)(lambda: act(lambda parity: lon_copy(parity, slab, 0)))
        pl.when(lon > 0)(lambda: act(lambda parity: lon_copy(parity, slab, 1)))
        pl.when((slab == slabs - 1) & (lev < levs - 1))(lambda: act(lambda parity: lev_copy(parity, 0)))
        pl.when((slab == 0) & (lev > 0))(lambda: act(lambda parity: lev_copy(parity, 1)))

    def send(parity, slab):
        lat_copy(parity, slab).start()
        to_sides(slab, lambda copy: copy(parity).start())

    def wait_sent(parity, slab):
        lat_copy(parity, slab).wait_send()
        to_sides(slab, lambda copy: copy(parity).wait_send())

    def wait_received(parity, slab):
        from_sides(slab, lambda copy: copy(parity).wait_recv())
        lat_copy(parity, slab).wait_recv()

    def after(parity, slab, row):
        xs = pl.ds(1, wide)
        start = pl.multiple_of((slab + 1) * TILE, TILE)
        middle = field[parity, row, xs, pl.ds(start, TILE)]
        around = field[parity, row, xs, pl.ds(start - 1, TILE)] + field[parity, row, xs, pl.ds(start + 1, TILE)]
        around += field[parity, row, pl.ds(0, wide), pl.ds(start, TILE)]
        around += field[parity, row, pl.ds(2, wide), pl.ds(start, TILE)]
        around += beyond[parity, :, inner(slab)] if row == 0 else field[parity, row - 1, xs, pl.ds(start, TILE)]
        if row < rows - 1:
            around += field[parity, row + 1, xs, pl.ds(start, TILE)]
        return middle * (0.6 - 0.2 * (middle * crowd[row, :, inner(slab)])) + 0.1 * around

    loads = []
    for row in range(rows):
        loads.append(
            pltpu.make_async_copy(
                density.at[own_row(row)],
                field.at[0, row, pl.ds(1, wide), pl.ds(TILE, deep)],
                load_sems.at[0, row],
            )
        )
    for row in range(rows):
        loads.append(pltpu.make_async_copy(crowding.at[own_row(row)], crowd.at[row], load_sems.at[1, row]))
    for load in loads:
        load.start()

    @pl.loop(0, rows)
    def _(row):
        for parity in range(2):
            for x in (0, wide + 1):
                field[parity, row, x] = jnp.zeros(field.shape[3:], jnp.float32)
            for z in (0, deep + TILE):
                field[parity, row, pl.ds(1, wide), pl.ds(z, TILE)] = jnp.zeros((wide, TILE, field.shape[4]), jnp.float32)

    barrier = pltpu.get_barrier_semaphore()

    def greet(there):
        pl.semaphore_signal(barrier, 1, device_id=there, device_id_type=MESH)

    greet({"lat": 1 - lat})
    for away in range(1, lons):
        greet({"lon": (lon + away) % lons})
    pl.when(lev > 0)(lambda: greet({"lev": lev - 1}))
    pl.when(lev < levs - 1)(lambda: greet({"lev": lev + 1}))
    pl.semaphore_wait(barrier, lons + jnp.minimum(lev, 1) + jnp.minimum(levs - 1 - lev, 1))

    for load in loads[:rows]:
        load.wait()

    @pl.loop(0, slabs)
    def _(place):
        send(0, slab_at(place))

    for load in loads[rows:]:
        load.wait()

    @pl.loop(0, (STEPS - 1) * slabs)
    def _(count):
        step, slab = count // slabs, slab_at(count % slabs)
        now, later = step % 2, (step + 1) % 2
        pl.when(step > 0)(lambda: wait_sent(later, slab))
        wait_received(now, slab)
        for row in range(rows):
            field[later, row, pl.ds(1, wide), padded(slab)] = after(now, slab, row)
        send(later, slab)

    last = (STEPS - 1) % 2
    total_wide = wide * lons

    def finish(slab):
        for away in range(1, lons):
            stat_copy(slab, lon, (lon + away) % lons).wait_recv()
        sums = [stats[slab, source, 0] for source in range(lons)]
        squares = [stats[slab, source, 1] for source in range(lons)]
        mean = sum(sums) * (1.0 / total_wide)
        spread = sum(squares)
        for part in sums:
            apart = part * (1.0 / wide) - mean
            spread += wide * (apart * apart)
        scale = lax.rsqrt(spread * (1.0 / total_wide) + 0.0001)
        for row in range(rows):
            value = density_out[own_row(row), :, inner(slab)]
            scaled_out[own_row(row), :, inner(slab)] = (value - mean[row][None]) * scale[row][None]

    lag = 2

    @pl.loop(0, slabs)
    def _(place):
        slab = slab_at(place)
        wait_received(last, slab)
        for row in range(rows):
            value = after(last, slab, row)
            density_out[own_row(row), :, inner(slab)] = value
            part = jnp.sum(value, axis=0)
            moved = value - (part * (1.0 / wide))[None]
            stats[slab, lon, 0, row] = part
            stats[slab, lon, 1, row] = jnp.sum(moved * moved, axis=0)
        for away in range(1, lons):
            stat_copy(slab, (lon + away) % lons, lon).start()
        pl.when(place >= lag)(lambda: finish(slab_at(place - lag)))

    for place in range(slabs - lag, slabs):
        finish(slab_at(place))

    @pl.loop(0, slabs)
    def _(slab):
        wait_sent(1 - last, slab)
        wait_sent(last, slab)
        for away in range(1, lons):
            stat_copy(slab, (lon + away) % lons, lon).wait_send()


def shards(density, crowding, *, devices):
    rows, wide, deep, species = density.shape
    slabs = deep // TILE
    dma = pltpu.SemaphoreType.DMA
    return pl.pallas_call(
        functools.partial(kernel, devices, density.shape),
        out_shape=[jax.ShapeDtypeStruct(density.shape, jnp.float32)] * 2,
        in_specs=[pl.BlockSpec(memory_space=pl.ANY)] * 2,
        out_specs=[pl.BlockSpec(memory_space=pltpu.VMEM)] * 2,
        scratch_shapes=[
            pltpu.VMEM((2, rows, wide + 2, deep + 2 * TILE, species), jnp.float32),
            pltpu.VMEM((rows, wide, deep, species), jnp.float32),
            pltpu.VMEM((2, wide, deep, species), jnp.float32),
            pltpu.VMEM((slabs, devices["lon"], 2, rows, TILE, species), jnp.float32),
            dma((2, rows)),
            dma((2, slabs)),
            dma((2, slabs)),
            dma((2, 2, slabs)),
            dma((2, 2, slabs)),
            dma((2, 2)),
            dma((2, 2)),
            dma((slabs, devices["lon"])),
            dma((slabs, devices["lon"])),
        ],
        compiler_params=pltpu.CompilerParams(
            collective_id=0, has_side_effects=True, vmem_limit_bytes=44 * 2**20
        ),
        name="growth",
    )(density, crowding)


def solution(mesh):
    placed = P(("trial", "lat"), "lon", "lev", None)
    return jax.shard_map(
        functools.partial(shards, devices=dict(mesh.shape)),
        mesh=mesh,
        in_specs=(placed, placed),
        out_specs=(placed, placed),
        check_vma=False,
    )
```

time: 276 us -> 207 us (0.75)
  Pallas kernels: 0 us -> 202 us
  starting transfers between devices: 118 us -> 0 us
  waiting for transfers between devices: 64.5 us -> 0 us
  other arithmetic: 41.9 us -> 0 us
  blocking collectives: 40.6 us -> 0 us
  local copies, waits for them, and re-layouts: 8.81 us -> 4.03 us
    pallas_call x0 -> x1, Pallas kernels: none -> 202 us  [shards(): pl.pallas_call(functools.partial(kernel, devices, density.shape), out_sha...]
    ppermute x24 -> x0, starting transfers between devices: 118 us -> none  [the longest x12 99.9 us: with_halo(): lax.ppermute(last, axis, up)]
    ppermute x24 -> x0, waiting for transfers between devices: 64.5 us -> none  [the longest x12 51.3 us: with_halo(): lax.ppermute(first, axis, [(b, a) for a, b in up])]
    all_to_all x1 -> x0, blocking collectives: 40.6 us -> none  [from_everyone(): lax.all_to_all(jnp.broadcast_to(array[None], (devices, *array.shape)), ax...]
    add x4 -> x0, other arithmetic: 25.4 us -> none  [the longest x3 25.3 us: advance(): return middle + 0.1 * spread + 0.2 * middle * (1.0 - middle * crowding)]
    reduce_sum x2 -> x0, other arithmetic: 11.4 us -> none  [the longest x1 9.51 us: shards(): jnp.sum(moved, axis=1, keepdims=True)]
    mul x1 -> x0, other arithmetic: 5.01 us -> none  [shards(): scaled_field = centred * lax.rsqrt(line_variance + 0.0001)]
  transfers between devices with their start and end apart: 24 -> 0, of which waited for: 12 -> 0; matrix products, arithmetic and copies ran while one was open for 2% -> 0% of each run, Pallas kernels for 0% -> 0%
where the time goes in v1:
time: 207 us
  Pallas kernels  202 us (98%)
  local copies, waits for them, and re-layouts  4.03 us (2%)
    pallas_call x1, Pallas kernels, shards(): pl.pallas_call(functools.partial(kernel, devices, density.shape), out_sha...  202 us

profile of v1, /device:TPU:1, one launch (start us, length us, event | category | flops | bytes accessed | tf_op | source)
XLA Modules:
  0.0 207.0 jit_solution(14375855269670804801)
XLA Ops:
  0.6 202.3 %growth.1 = (f32[4,16,128,128]{3,2,1,0:T(8,128)S(1)}, f32[4,16,128,128]{3,2,1,0:T(8,128)S(1)}) custom-call(f32[4,16,128,128]{3,2,1,0:T(8,128)} %density.1, f32[4,16,128,128]{3,2,1,0:T(8,128)} %crowding.1), custom_call_target="tpu_custom_call" | custom-call | tf_op jit(solution)/shard_map/growth/pallas_call | solution.py:218
  203.0 2.0 copy.6
  205.0 2.0 copy.7

commit v2 on v1

v2 whole, which is shorter than its diff:
```python
import functools

import jax
import jax.numpy as jnp
from jax import lax
from jax.experimental import pallas as pl
from jax.experimental.pallas import tpu as pltpu
from jax.sharding import PartitionSpec as P

STEPS = 4
TILE = 8
AHEAD_A = 12
AHEAD_B = 12
BUNCH = 4
MESH = pl.DeviceIdType.MESH


def bunches_of_places(slabs):
    at, bunches = 0, []
    while slabs - at > 1:
        bunches.append((at, (slabs - at) // 2))
        at += (slabs - at) // 2
    return [*bunches, (at, 1)]


def kernel(
    devices, shape, density, crowding, scaled_out, density_out,
    field, crowd, beyond, stats, load_sems, ready,
    lat_send, lat_recv, lon_send, lon_recv, lev_send, lev_recv, stat_send, stat_recv,
):
    rows, wide, deep, _ = shape
    slabs = deep // TILE
    trial = lax.axis_index("trial")
    ahead = AHEAD_A - (AHEAD_A - AHEAD_B) * (trial // 2)
    half = slabs // 2
    lat, lon, lev = (lax.axis_index(a) for a in ("lat", "lon", "lev"))
    lons, levs = devices["lon"], devices["lev"]
    sides = lons - 1 + jnp.minimum(lev, 1) + jnp.minimum(levs - 1 - lev, 1)
    bunches = bunches_of_places(slabs)

    def own_row(row):
        return lat * row + (1 - lat) * (rows - 1 - row)

    def slab_at(place):
        bunch = place // BUNCH
        odd = bunch % 2
        return (odd * (slabs // BUNCH - 1) + (1 - 2 * odd) * (bunch // 2)) * BUNCH + place % BUNCH

    def inner(slab):
        return pl.ds(pl.multiple_of(slab * TILE, TILE), TILE)

    def padded(slab, number=1):
        return pl.ds(pl.multiple_of((slab + 1) * TILE, TILE), number * TILE)

    def lat_copy(count):
        place = count % slabs
        slab = slab_at(place)
        return pltpu.make_async_remote_copy(
            src_ref=field.at[count // slabs % 2, 0, pl.ds(1, wide), padded(slab)],
            dst_ref=beyond.at[count // slabs % 2, :, inner(slab)],
            send_sem=lat_send.at[place],
            recv_sem=lat_recv.at[count // slabs % 2, place],
            device_id={"lat": 1 - lat},
            device_id_type=MESH,
        )

    def lon_copy(parity, first, up):
        cells = padded(first, BUNCH)
        return pltpu.make_async_remote_copy(
            src_ref=field.at[parity, :, wide if up else 1, cells],
            dst_ref=field.at[parity, :, 0 if up else wide + 1, cells],
            send_sem=lon_send.at[up, parity, first // BUNCH],
            recv_sem=lon_recv.at[up, parity, first // BUNCH],
            device_id={"lon": lon + (1 if up else -1)},
            device_id_type=MESH,
        )

    def lev_copy(parity, up):
        return pltpu.make_async_remote_copy(
            src_ref=field.at[parity, :, pl.ds(1, wide), pl.ds(deep if up else TILE, TILE)],
            dst_ref=field.at[parity, :, pl.ds(1, wide), pl.ds(0 if up else deep + TILE, TILE)],
            send_sem=lev_send.at[up, parity],
            recv_sem=lev_recv.at[up, parity],
            device_id={"lev": lev + (1 if up else -1)},
            device_id_type=MESH,
        )

    def on_both_sides(place, act, out, at):
        slab = slab_at(place)
        first = slab - at
        turn = place % BUNCH == at
        pl.when(turn & (lon > 0))(lambda: act(lambda parity: lon_copy(parity, first, 0 if out else 1)))
        pl.when(turn & (lon < lons - 1))(lambda: act(lambda parity: lon_copy(parity, first, 1 if out else 0)))
        pl.when((slab == 0) & (lev > 0))(lambda: act(lambda parity: lev_copy(parity, 0 if out else 1)))
        pl.when((slab == slabs - 1) & (lev < levs - 1))(lambda: act(lambda parity: lev_copy(parity, 1 if out else 0)))

    def send_sides(parity, place):
        on_both_sides(place, lambda copy: copy(parity).start(), True, BUNCH - 1)

    def wait_sent_sides(parity, place):
        on_both_sides(place, lambda copy: copy(parity).wait_send(), True, 0)

    def wait_sides(parity, place):
        on_both_sides(place, lambda copy: copy(parity).wait_recv(), False, 0)

    def send_ahead(count):
        later = count + ahead

        def send():
            pl.when(later >= slabs)(lambda: lat_copy(later - slabs).wait_send())
            lat_copy(later).start()

        pl.when(later < STEPS * slabs)(send)

    def after(parity, slab, row):
        xs = pl.ds(1, wide)
        start = pl.multiple_of((slab + 1) * TILE, TILE)
        middle = field[parity, row, xs, pl.ds(start, TILE)]
        before = field[parity, row, xs, padded(slab - 1)]
        behind = field[parity, row, xs, padded(slab + 1)]
        z = lax.broadcasted_iota(jnp.int32, middle.shape, 1)
        around = pltpu.roll(jnp.where(z == TILE - 1, before, middle), 1, 1)
        around += pltpu.roll(jnp.where(z == 0, behind, middle), TILE - 1, 1)
        around += field[parity, row, pl.ds(0, wide), pl.ds(start, TILE)]
        around += field[parity, row, pl.ds(2, wide), pl.ds(start, TILE)]
        around += beyond[parity, :, inner(slab)] if row == 0 else field[parity, row - 1, xs, pl.ds(start, TILE)]
        if row < rows - 1:
            around += field[parity, row + 1, xs, pl.ds(start, TILE)]
        return middle * (0.6 - 0.2 * (middle * crowd[row, :, inner(slab)])) + 0.1 * around

    barrier = pltpu.get_barrier_semaphore()

    def tell(semaphore, there):
        pl.semaphore_signal(semaphore, 1, device_id=there, device_id_type=MESH)

    def tell_sides(semaphore):
        for away in range(1, lons):
            tell(semaphore, {"lon": (lon + away) % lons})
        pl.when(lev > 0)(lambda: tell(semaphore, {"lev": lev - 1}))
        pl.when(lev < levs - 1)(lambda: tell(semaphore, {"lev": lev + 1}))

    def load_field(row):
        into = field.at[0, row, pl.ds(1, wide), pl.ds(TILE, deep)]
        return pltpu.make_async_copy(density.at[own_row(row)], into, load_sems.at[min(row, 1)])

    def load_crowd(row):
        return pltpu.make_async_copy(crowding.at[own_row(row)], crowd.at[row], load_sems.at[2])

    load_field(0).start()
    tell(barrier, {"lat": 1 - lat})
    pl.when(lat == 0)(lambda: tell_sides(barrier))
    load_field(0).wait()
    for row in range(1, rows):
        load_field(row).start()
    for row in range(rows):
        load_crowd(row).start()
    pl.semaphore_wait(barrier, 1 + (1 - lat) * sides)

    @pl.loop(0, ahead)
    def _(count):
        send_ahead(count - ahead)

    pl.when(lat == 0)(lambda: tell_sides(ready))

    def clear(row, x, z):
        for parity in range(2):
            field[parity, row, x, z] = jnp.zeros_like(field[parity, row, x, z])

    @pl.loop(0, rows)
    def _(row):
        pl.when(lon == 0)(lambda: clear(row, pl.ds(0, 1), pl.ds(0, deep + 2 * TILE)))
        pl.when(lon == lons - 1)(lambda: clear(row, pl.ds(wide + 1, 1), pl.ds(0, deep + 2 * TILE)))
        pl.when(lev == 0)(lambda: clear(row, pl.ds(1, wide), pl.ds(0, TILE)))
        pl.when(lev == levs - 1)(lambda: clear(row, pl.ds(1, wide), pl.ds(deep + TILE, TILE)))

    pl.semaphore_wait(ready, lat + (1 - lat) * sides)
    pl.when(lat == 0)(lambda: tell(ready, {"lat": 1}))
    others = pl.ds(1, rows - 1)
    pltpu.make_async_copy(
        density.at[others], field.at[0, others, pl.ds(1, wide), pl.ds(TILE, deep)], load_sems.at[1]
    ).wait()

    @pl.loop(0, slabs)
    def _(place):
        send_sides(0, place)

    pltpu.make_async_copy(crowding, crowd, load_sems.at[2]).wait()

    @pl.loop(0, (STEPS - 1) * slabs)
    def _(count):
        step, place = count // slabs, count % slabs
        slab = slab_at(place)
        now, later = step % 2, (step + 1) % 2
        pl.when(step > 0)(lambda: wait_sent_sides(later, place))
        wait_sides(now, place)
        lat_copy(count).wait_recv()
        for row in range(rows):
            field[later, row, pl.ds(1, wide), padded(slab)] = after(now, slab, row)
        send_sides(later, place)
        send_ahead(count)

    last = (STEPS - 1) % 2
    total_wide = wide * lons

    def stat_copy(sem, first, number, near, peer):
        part = stats.at[pl.ds(first, number), lon, pl.ds(0, 1) if near else pl.ds(1, rows - 1)]
        return pltpu.make_async_remote_copy(
            src_ref=part,
            dst_ref=part,
            send_sem=stat_send.at[0],
            recv_sem=stat_recv.at[sem],
            device_id={"lon": peer},
            device_id_type=MESH,
        )

    def send_stats(sem, first, number, near):
        for away in range(1, lons):
            stat_copy(sem, first, number, near, (lon + away) % lons).start()

    def wait_stats(sem, first, number, near):
        part = stats.at[pl.ds(first, number), pl.ds(0, lons - 1), pl.ds(0, 1) if near else pl.ds(1, rows - 1)]
        pltpu.make_async_remote_copy(
            src_ref=part,
            dst_ref=part,
            send_sem=stat_send.at[0],
            recv_sem=stat_recv.at[sem],
            device_id={"lon": lon},
            device_id_type=MESH,
        ).wait_recv()

    def close(row, place):
        slab = slab_at(place)
        value = after(last, slab, row)
        density_out[own_row(row), :, inner(slab)] = value
        part = jnp.sum(value, axis=0)
        moved = value - (part * (1.0 / wide))[None]
        stats[place, lon, row, 0] = part
        stats[place, lon, row, 1] = jnp.sum(moved * moved, axis=0)

    def finish(row, place):
        slab = slab_at(place)
        sums = [stats[place, source, row, 0] for source in range(lons)]
        mean = sum(sums) * (1.0 / total_wide)
        spread = sum(stats[place, source, row, 1] for source in range(lons))
        for part in sums:
            apart = part * (1.0 / wide) - mean
            spread += wide * (apart * apart)
        scale = lax.rsqrt(spread * (1.0 / total_wide) + 0.0001)
        value = density_out[own_row(row), :, inner(slab)]
        scaled_out[own_row(row), :, inner(slab)] = (value - mean[None]) * scale[None]

    @pl.loop(0, slabs)
    def _(place):
        wait_sides(last, place)
        for row in range(1, rows):
            close(row, place)
        for part in range(2):
            pl.when(place == (part + 1) * half - 1)(lambda: send_stats(part, part * half, half, False))

    @pl.loop(0, slabs)
    def _(place):
        lat_copy((STEPS - 1) * slabs + place).wait_recv()
        close(0, place)
        for which, (first, number) in enumerate(bunches):
            pl.when(place == first + number - 1)(lambda: send_stats(2 + which, first, number, True))
        send_ahead((STEPS - 1) * slabs + place)
        for part in range(2):
            pl.when(place == half + part * half // 2)(lambda: wait_stats(part, part * half, half, False))

        @pl.when(place >= half)
        def _():
            for more in range(2):
                for row in range(1, rows):
                    finish(row, 2 * (place - half) + more)

        pl.when(place == slabs - half // 2)(lambda: wait_stats(2, *bunches[0], True))

        @pl.when(place >= slabs - half // 2)
        def _():
            for more in range(2):
                finish(0, 2 * (place - slabs + half // 2) + more)

    @pl.loop(0, slabs)
    def _(place):
        wait_sent_sides(1 - last, place)
        wait_sent_sides(last, place)
        lat_copy((STEPS - 1) * slabs + place).wait_send()

    for which, (first, number) in enumerate(bunches):
        if which > 0:
            wait_stats(2 + which, first, number, True)

            @pl.loop(first, first + number)
            def _(place):
                finish(0, place)

    part = stats.at[:, pl.ds(0, lons - 1)]
    pltpu.make_async_remote_copy(
        src_ref=part,
        dst_ref=part,
        send_sem=stat_send.at[0],
        recv_sem=stat_recv.at[0],
        device_id={"lon": lon},
        device_id_type=MESH,
    ).wait_send()


def shards(density, crowding, *, devices):
    rows, wide, deep, species = density.shape
    slabs = deep // TILE
    dma = pltpu.SemaphoreType.DMA
    return pl.pallas_call(
        functools.partial(kernel, devices, density.shape),
        out_shape=[jax.ShapeDtypeStruct(density.shape, jnp.float32)] * 2,
        in_specs=[pl.BlockSpec(memory_space=pl.ANY)] * 2,
        out_specs=[pl.BlockSpec(memory_space=pltpu.VMEM)] * 2,
        scratch_shapes=[
            pltpu.VMEM((2, rows, wide + 2, deep + 2 * TILE, species), jnp.float32),
            pltpu.VMEM((rows, wide, deep, species), jnp.float32),
            pltpu.VMEM((2, wide, deep, species), jnp.float32),
            pltpu.VMEM((slabs, devices["lon"], rows, 2, TILE, species), jnp.float32),
            dma((3,)),
            pltpu.SemaphoreType.REGULAR,
            dma((slabs,)),
            dma((2, slabs)),
            dma((2, 2, slabs // BUNCH)),
            dma((2, 2, slabs // BUNCH)),
            dma((2, 2)),
            dma((2, 2)),
            dma((1,)),
            dma((2 + len(bunches_of_places(slabs)),)),
        ],
        compiler_params=pltpu.CompilerParams(
            collective_id=0, has_side_effects=True, vmem_limit_bytes=44 * 2**20
        ),
        name="growth",
    )(density, crowding)


def solution(mesh):
    placed = P(("trial", "lat"), "lon", "lev", None)
    return jax.shard_map(
        functools.partial(shards, devices=dict(mesh.shape)),
        mesh=mesh,
        in_specs=(placed, placed),
        out_specs=(placed, placed),
        check_vma=False,
    )
```

time: 207 us -> 202 us (0.976)
  Pallas kernels: 202 us -> 197 us
    pallas_call x1, Pallas kernels: 202 us -> 197 us  [shards(): pl.pallas_call(functools.partial(kernel, devices, density.shape), out_sha...]
where the time goes in v2:
time: 202 us
  Pallas kernels  197 us (98%)
  local copies, waits for them, and re-layouts  4.03 us (2%)
    pallas_call x1, Pallas kernels, shards(): pl.pallas_call(functools.partial(kernel, devices, density.shape), out_sha...  197 us

profile of v2, /device:TPU:1, one launch (start us, length us, event | category | flops | bytes accessed | tf_op | source)
XLA Modules:
  0.0 202.0 jit_solution(10335963605008286424)
XLA Ops:
  0.6 197.3 %growth.1 = (f32[4,16,128,128]{3,2,1,0:T(8,128)S(1)}, f32[4,16,128,128]{3,2,1,0:T(8,128)S(1)}) custom-call(f32[4,16,128,128]{3,2,1,0:T(8,128)} %density.1, f32[4,16,128,128]{3,2,1,0:T(8,128)} %crowding.1), custom_call_target="tpu_custom_call" | custom-call | tf_op jit(solution)/shard_map/growth/pallas_call | solution.py:312
  198.0 2.0 copy.6
  200.0 2.0 copy.7

commit v3 on v2

--- a/solution.py
+++ b/solution.py
@@ -77,8 +77,8 @@
 
     def lev_copy(parity, up):
         return pltpu.make_async_remote_copy(
-            src_ref=field.at[parity, :, pl.ds(1, wide), pl.ds(deep if up else TILE, TILE)],
-            dst_ref=field.at[parity, :, pl.ds(1, wide), pl.ds(0 if up else deep + TILE, TILE)],
+            src_ref=field.at[parity, :, pl.ds(1, wide), pl.ds(deep + TILE - 1 if up else TILE, 1)],
+            dst_ref=field.at[parity, :, pl.ds(1, wide), pl.ds(TILE - 1 if up else deep + TILE, 1)],
             send_sem=lev_send.at[up, parity],
             recv_sem=lev_recv.at[up, parity],
             device_id={"lev": lev + (1 if up else -1)},
@@ -305,11 +305,22 @@
     ).wait_send()
 
 
+def deliver(scaled, density, scaled_out, density_out, sems):
+    copies = []
+    for part, (held, out) in enumerate(((scaled, scaled_out), (density, density_out))):
+        for row in range(held.shape[0]):
+            copies.append(pltpu.make_async_copy(held.at[row], out.at[row], sems.at[part, row]))
+    for copy in copies:
+        copy.start()
+    for copy in copies:
+        copy.wait()
+
+
 def shards(density, crowding, *, devices):
     rows, wide, deep, species = density.shape
     slabs = deep // TILE
     dma = pltpu.SemaphoreType.DMA
-    return pl.pallas_call(
+    held = pl.pallas_call(
         functools.partial(kernel, devices, density.shape),
         out_shape=[jax.ShapeDtypeStruct(density.shape, jnp.float32)] * 2,
         in_specs=[pl.BlockSpec(memory_space=pl.ANY)] * 2,
@@ -335,6 +346,15 @@
         ),
         name="growth",
     )(density, crowding)
+    return pl.pallas_call(
+        deliver,
+        out_shape=[jax.ShapeDtypeStruct(density.shape, jnp.float32)] * 2,
+        in_specs=[pl.BlockSpec(memory_space=pltpu.VMEM)] * 2,
+        out_specs=[pl.BlockSpec(memory_space=pl.ANY)] * 2,
+        scratch_shapes=[dma((2, rows))],
+        compiler_params=pltpu.CompilerParams(vmem_limit_bytes=44 * 2**20),
+        name="deliver",
+    )(*held)
 
 
 def solution(mesh):

time: 202 us -> 201 us (level)
  local copies, waits for them, and re-layouts: 4.03 us -> 0 us
  Pallas kernels: 197 us -> 201 us
    unnamed x2 -> x0, local copies, waits for them, and re-layouts: 4.03 us -> none
    pallas_call x0 -> x1, Pallas kernels: none -> 3.37 us  [shards(): pl.pallas_call(deliver, out_shape=[jax.ShapeDtypeStruct(density.shape, jn...]
where the time goes in v3:
time: 201 us
  Pallas kernels  201 us (100%)
    pallas_call x1, Pallas kernels, shards(): pl.pallas_call(functools.partial(kernel, devices, density.shape), out_sha...  197 us

profile of v3, /device:TPU:1, one launch (start us, length us, event | category | flops | bytes accessed | tf_op | source)
XLA Modules:
  0.0 201.3 jit_solution(11168052224254180390)
XLA Ops:
  0.6 197.3 %growth.1 = (f32[4,16,128,128]{3,2,1,0:T(8,128)S(1)}, f32[4,16,128,128]{3,2,1,0:T(8,128)S(1)}) custom-call(f32[4,16,128,128]{3,2,1,0:T(8,128)} %density.1, f32[4,16,128,128]{3,2,1,0:T(8,128)} %crowding.1), custom_call_target="tpu_custom_call" | custom-call | tf_op jit(solution)/shard_map/growth/pallas_call | solution.py:323
  198.0 3.4 %deliver.1 = (f32[4,16,128,128]{3,2,1,0:T(8,128)}, f32[4,16,128,128]{3,2,1,0:T(8,128)}) custom-call(f32[4,16,128,128]{3,2,1,0:T(8,128)S(1)} %get-tuple-element.4.scaled, f32[4,16,128,128]{3,2,1,0:T(8,128)S(1)} %get-tuple-element.5.density), custom_call_target="tpu_custom_call" | custom-call | tf_op jit(solution)/shard_map/deliver/pallas_call | solution.py:349

commit v4 on v3

--- a/solution.py
+++ b/solution.py
@@ -46,19 +46,19 @@
         odd = bunch % 2
         return (odd * (slabs // BUNCH - 1) + (1 - 2 * odd) * (bunch // 2)) * BUNCH + place % BUNCH
 
-    def inner(slab):
-        return pl.ds(pl.multiple_of(slab * TILE, TILE), TILE)
+    def inner(slab, number=1):
+        return pl.ds(pl.multiple_of(slab * TILE, TILE), number * TILE)
 
     def padded(slab, number=1):
         return pl.ds(pl.multiple_of((slab + 1) * TILE, TILE), number * TILE)
 
-    def lat_copy(count):
+    def lat_copy(count, number=1):
         place = count % slabs
         slab = slab_at(place)
         return pltpu.make_async_remote_copy(
-            src_ref=field.at[count // slabs % 2, 0, pl.ds(1, wide), padded(slab)],
-            dst_ref=beyond.at[count // slabs % 2, :, inner(slab)],
-            send_sem=lat_send.at[place],
+            src_ref=field.at[count // slabs % 2, 0, pl.ds(1, wide), padded(slab, number)],
+            dst_ref=beyond.at[count // slabs % 2, :, inner(slab, number)],
+            send_sem=lat_send.at[place // BUNCH],
             recv_sem=lat_recv.at[count // slabs % 2, place],
             device_id={"lat": 1 - lat},
             device_id_type=MESH,
@@ -107,7 +107,8 @@
         later = count + ahead
 
         def send():
-            pl.when(later >= slabs)(lambda: lat_copy(later - slabs).wait_send())
+            turn = (later >= slabs) & (later % BUNCH == 0)
+            pl.when(turn)(lambda: lat_copy(later - slabs, BUNCH).wait_send())
             lat_copy(later).start()
 
         pl.when(later < STEPS * slabs)(send)
@@ -284,7 +285,8 @@
     def _(place):
         wait_sent_sides(1 - last, place)
         wait_sent_sides(last, place)
-        lat_copy((STEPS - 1) * slabs + place).wait_send()
+        turn = place % BUNCH == 0
+        pl.when(turn)(lambda: lat_copy((STEPS - 1) * slabs + place, BUNCH).wait_send())
 
     for which, (first, number) in enumerate(bunches):
         if which > 0:
@@ -332,7 +334,7 @@
             pltpu.VMEM((slabs, devices["lon"], rows, 2, TILE, species), jnp.float32),
             dma((3,)),
             pltpu.SemaphoreType.REGULAR,
-            dma((slabs,)),
+            dma((slabs // BUNCH,)),
             dma((2, slabs)),
             dma((2, 2, slabs // BUNCH)),
             dma((2, 2, slabs // BUNCH)),

time: 201 us -> 201 us (level)
  no operation moved by 1% of the time
where the time goes in v4:
time: 201 us
  Pallas kernels  201 us (100%)
    pallas_call x1, Pallas kernels, shards(): pl.pallas_call(functools.partial(kernel, devices, density.shape), out_sha...  197 us

profile of v4, /device:TPU:1, one launch (start us, length us, event | category | flops | bytes accessed | tf_op | source)
XLA Modules:
  0.0 201.2 jit_solution(11732733356960230773)
XLA Ops:
  0.6 197.2 %growth.1 = (f32[4,16,128,128]{3,2,1,0:T(8,128)S(1)}, f32[4,16,128,128]{3,2,1,0:T(8,128)S(1)}) custom-call(f32[4,16,128,128]{3,2,1,0:T(8,128)} %density.1, f32[4,16,128,128]{3,2,1,0:T(8,128)} %crowding.1), custom_call_target="tpu_custom_call" | custom-call | tf_op jit(solution)/shard_map/growth/pallas_call | solution.py:325
  197.8 3.4 %deliver.1 = (f32[4,16,128,128]{3,2,1,0:T(8,128)}, f32[4,16,128,128]{3,2,1,0:T(8,128)}) custom-call(f32[4,16,128,128]{3,2,1,0:T(8,128)S(1)} %get-tuple-element.4.scaled, f32[4,16,128,128]{3,2,1,0:T(8,128)S(1)} %get-tuple-element.5.density), custom_call_target="tpu_custom_call" | custom-call | tf_op jit(solution)/shard_map/deliver/pallas_call | solution.py:351
